TPU v7x, 32 devices: a whole 2x2x4 slice. The times are simulated.
32 devices in a mesh: expert: 4 (over x, core), row: 2 (over y), col: 4 (over z).
Axes of the slice: x: 2, y: 2, z: 4, core: 2. Of those that a mesh axis runs over, the one named last changes fastest.
Arguments:
- weights: bfloat16 [4, 4096, 7168], P('expert', 'row', 'col'), may hold values from -210 to 210
- inputs: bfloat16 [4, 1024, 4096], P('expert', ('row', 'col')), may hold values from -80 to 80
- cotangents: bfloat16 [4, 1024, 7168], P('expert', ('row', 'col')), may hold values from -150 to 150
- row_state: float32 [4, 4096], P('expert', 'row'), may hold values from 0.00089 to 0.91
- col_state: float32 [4, 7168], P('expert', 'col'), may hold values from 0.00089 to 0.91
Outputs:
- scaled_update: float32 [4, 4096, 7168], P('expert', 'row', 'col')
- new_row_state: float32 [4, 4096], P('expert', 'row')
- new_col_state: float32 [4, 7168], P('expert', 'col')
All inputs are finite; a program needn't handle non-finite values.
Results may differ from a plain program's by a relative error of at most 0.0003.
Values may be sent and summed in bfloat16 or wider, within the bound.
A program may use at most 128 MiB of HBM per device.

v0:
```python
import jax
import jax.numpy as jnp
from jax import lax
from jax.sharding import PartitionSpec as P

STEP = 10
eps_square = 1e-30


def reduce_factors(row_part, col_part):
    row_total = lax.psum(row_part, "col")
    col_total = lax.psum(col_part, "row")
    return (row_total, col_total)


def body(weights, inputs, cotangents, row_state, col_state):
    matrices, rows_here, cols_here = weights.shape
    model_width = inputs.shape[2]
    hidden_width = cotangents.shape[2]
    row_count = lax.axis_size("row")
    col_count = lax.axis_size("col")
    block_rows = inputs.shape[1]
    inputs_split = lax.all_to_all(inputs, "row", split_axis=2, concat_axis=1, tiled=True)
    hidden_split = lax.all_to_all(cotangents, "col", split_axis=2, concat_axis=1, tiled=True)
    hidden_all = lax.all_gather(hidden_split, "row", axis=1, tiled=True)
    hidden_blocks = hidden_all.reshape(matrices, row_count, col_count, block_rows, cols_here)
    shard_rows = lax.all_gather(inputs_split, "col", axis=1, tiled=True)
    block_count = shard_rows.shape[1] // (row_count * block_rows)
    input_blocks = shard_rows.reshape(matrices, block_count, row_count, block_rows, rows_here)
    gradient = jnp.einsum(
        "mkrti,mrktj->mij", input_blocks, hidden_blocks, preferred_element_type=jnp.float32
    )
    decay_rate = 1.0 - STEP ** (-0.8)
    entry_count = model_width * hidden_width
    squares = gradient * gradient
    weights_wide = weights.astype(jnp.float32)
    weight_squares = jnp.sum(weights_wide * weights_wide, axis=(1, 2))
    squared_total = lax.psum(jnp.sum(squares), ("expert", "row", "col"))
    clip_scale = 1.0 / jnp.maximum(
        1.0, jnp.sqrt(squared_total / (matrices * lax.axis_size("expert") * entry_count))
    )
    clipped = clip_scale * gradient
    clipped_squares = clipped * clipped + eps_square
    row_sum, col_sum = reduce_factors(
        jnp.sum(clipped_squares, axis=2), jnp.sum(clipped_squares, axis=1)
    )
    new_rows = decay_rate * row_state + (1.0 - decay_rate) * (row_sum / hidden_width)
    new_cols = decay_rate * col_state + (1.0 - decay_rate) * (col_sum / model_width)
    row_average = lax.psum(jnp.sum(new_rows, axis=1), "row") / model_width
    second = new_rows[:, :, None] * new_cols[:, None, :] / row_average[:, None, None]
    update = clipped / jnp.sqrt(second)
    update_squares = jnp.sum(update * update, axis=(1, 2))
    update_total, weight_total = lax.psum((update_squares, weight_squares), ("row", "col"))
    update = update / jnp.maximum(1.0, jnp.sqrt(update_total / entry_count))[:, None, None]
    weight_rms = jnp.sqrt(weight_total / entry_count)
    return (weight_rms[:, None, None] * update, new_rows, new_cols)


def solution(mesh):
    in_specs = (
        P("expert", "row", "col"),
        P("expert", ("row", "col"), None),
        P("expert", ("row", "col"), None),
        P("expert", "row"),
        P("expert", "col"),
    )
    out_specs = (P("expert", "row", "col"), P("expert", "row"), P("expert", "col"))
    return jax.shard_map(body, mesh=mesh, in_specs=in_specs, out_specs=out_specs, check_vma=False)
```

profile of v0, /device:TPU:0, one launch (start us, length us, event | category | flops | bytes accessed | tf_op | source)
XLA Modules:
  0.0 391.4 jit_solution(717447790940742205)
XLA Ops:
  7.2 0.0 all-gather.5.cloned.1.call-start
  7.2 8.6 %copy.18 = bf16[1,128,7168]{1,0,2:T(2,128)(2,1)} copy(bf16[1,128,7168]{2,1,0:T(8,128)(2,1)} %param.7) | data formatting | bytes 3670016 | tf_op args[2]
  15.8 0.5 broadcast.17
  16.3 41.1 %reduce.13 = bf16[7168,128]{1,0:T(8,128)(2,1)} reduce(bf16[7168,1,128]{2,1,0:T(2,128)(2,1)} %bitcast.44, bf16[]{:T(256)} %broadcast.17), dimensions={1}, to_apply=%bitcast.41.reduce_sub_computation | reduce | bytes 3670018
  57.4 2.5 reshape.55
  59.9 48.8 %all_to_all.36 = bf16[4,2,114688]{2,1,0:T(2,128)(2,1)} all-to-all(bf16[4,2,114688]{2,1,0:T(2,128)(2,1)S(1)} %reshape.55), channel_id=1, replica_groups=mesh['expert'=4,'row'=2,'col'=4] {'col'}, dimensions={0} | all-to-all | bytes 3670016 | tf_op jit(solution)/shard_map/all_to_all | solution.py:24
  108.7 4.7 %reshape.56 = bf16[7168,1,128]{2,1,0:T(2,128)(2,1)} reshape(bf16[4,2,114688]{2,1,0:T(2,128)(2,1)} %all_to_all.36) | data formatting | bytes 3670016
  113.4 2.3 copy.25
  115.7 2.4 copy.19
  118.1 0.0 all-gather.5.cloned.1.call-update
  118.1 0.2 all-gather.3.cloned.1.call-start
  118.4 2.8 copy.16
  121.2 22.4 %reduce.12 = bf16[4096,128]{1,0:T(8,128)(2,1)S(1)} reduce(bf16[4096,1,128]{2,1,0:T(2,128)(2,1)S(1)} %bitcast.47, bf16[]{:T(256)} %broadcast.17), dimensions={1}, to_apply=%bitcast.39.reduce_sub_computation | reduce | bytes 2097154
  143.6 0.3 reshape.53
  143.9 28.1 %all_to_all.37 = bf16[2,2,131072]{2,1,0:T(2,128)(2,1)S(1)} all-to-all(bf16[2,2,131072]{2,1,0:T(2,128)(2,1)S(1)} %reshape.53), channel_id=1, replica_groups=mesh['expert'=4,'row'=2,'col'=4] {'row'}, dimensions={0} | all-to-all | bytes 2097152 | tf_op jit(solution)/shard_map/all_to_all | solution.py:23
  172.0 0.9 reshape.54
  173.0 0.1 copy.24
  173.1 1.4 copy.17
  174.5 0.0 all-gather.3.cloned.1.call-update
  174.5 7.5 %multiply_reduce_fusion.1 = f32[]{:T(128)} fusion(bf16[1,2048,1792]{2,1,0:T(8,128)(2,1)} %param.5), kind=kLoop, calls=%fused_computation.7 | loop fusion | flops 11010047 | bytes 7340036 | tf_op jit(solution)/shard_map/reduce_sum | solution.py:37
  182.0 79.9 %all-gather.3.cloned.1.call-done = bf16[1,1024,2048]{2,1,0:T(8,128)(2,1)} async-done(((bf16[1,256,2048]{2,1,0:T(8,128)(2,1)}), bf16[1,1024,2048]{2,1,0:T(8,128)(2,1)}) %all-gather.3.cloned.1.call-update) | async-done | bytes 4194320 | tf_op jit(solution)/shard_map/all_gather | solution.py:27
  261.9 15.2 %fusion = (f32[]{:T(128)}, f32[2048,1792,1,1]{1,0,3,2:T(8,128)}) fusion(bf16[4,2,128,2048]{3,2,1,0:T(8,128)(2,1)} %bitcast.55, bf16[2,4,128,1792]{3,2,1,0:T(8,128)(2,1)} %bitcast.56), kind=kOutput, calls=%fused_computation.2 | convolution fusion | flops 7523532800 | bytes 22544388 | tf_op jit(solution)/shard_map/mkrti,mrktj->mij/dot_general | solution.py:30
  277.1 38.9 %psum.43 = f32[]{:T(128)} all-reduce(f32[]{:T(128)} %get-tuple-element.13), channel_id=1, replica_groups=mesh['expert'=4,'row'=2,'col'=4] {'expert','row','col'}, use_global_device_ids=true, to_apply=%region_3.0 | all-reduce | flops 1 | bytes 8 | tf_op jit(solution)/shard_map/psum | solution.py:38
  316.7 8.1 %fusion.1 = (f32[1792]{0:T(1024)S(1)}, f32[2048]{0:T(1024)S(1)}) fusion(f32[2048,1792,1,1]{1,0,3,2:T(8,128)} %get-tuple-element.14, f32[]{:T(128)S(6)} %div.46), kind=kLoop, calls=%fused_computation.8 | loop fusion | flops 18346240 | bytes 14695428 | tf_op jit(solution)/shard_map/reduce_sum | solution.py:45
  324.8 10.8 %psum.44 = f32[1,2048]{1,0:T(1,128)S(1)} all-reduce(f32[1,2048]{1,0:T(1,128)S(1)} %bitcast.54), channel_id=1, replica_groups=mesh['expert'=4,'row'=2,'col'=4] {'col'}, use_global_device_ids=true, to_apply=%region_5.0 | all-reduce | flops 2048 | bytes 16384 | tf_op jit(solution)/shard_map/psum | solution.py:11
  335.6 0.0 copy-done.2
  335.6 0.6 fusion.6
  336.2 6.0 %all-reduce.1 = (f32[1]{0:T(128)}, f32[1,1792]{1,0:T(1,128)S(1)}) all-reduce(f32[1]{0:T(128)} %bitcast.12, f32[1,1792]{1,0:T(1,128)S(1)} %reduce_sum.70), channel_id=1, replica_groups=mesh['expert'=4,'row'=2,'col'=4] {'row'}, use_global_device_ids=true, to_apply=%region_9.0 | all-reduce | flops 1793 | bytes 14344 | tf_op jit(solution)/shard_map/psum | solution.py:49
  342.9 0.6 fusion.5
  343.6 8.9 %multiply_reduce_fusion = f32[]{:T(128)} fusion(f32[]{:T(128)} %bitcast.13, f32[1792]{0:T(1024)S(1)} %get-tuple-element.9, f32[2048]{0:T(1024)S(1)} %bitcast.52, f32[2048,1792,1,1]{1,0,3,2:T(8,128)} %get-tuple-element.14, f32[]{:T(128)S(6)} %div.46), kind=kLoop, calls=%fused_computation.4 | loop fusion | flops 22020096 | bytes 14695436 | tf_op jit(solution)/shard_map/reduce_sum | solution.py:52
  352.4 19.1 %all-reduce = (f32[1]{0:T(128)}, f32[1]{0:T(128)}) all-reduce(f32[1]{0:T(128)} %bitcast.14, f32[1]{0:T(128)} %bitcast), channel_id=1, replica_groups=mesh['expert'=4,'row'=2,'col'=4] {'row','col'}, use_global_device_ids=true, to_apply=%region_11.0 | all-reduce | flops 2 | bytes 16 | tf_op jit(solution)/shard_map/psum | solution.py:53
  372.8 11.8 %multiply_bitcast_fusion = f32[1,2048,1792]{2,1,0:T(8,128)} fusion(f32[]{:T(128)} %bitcast.15, f32[]{:T(128)} %bitcast.1, f32[]{:T(128)} %bitcast.13, f32[1792]{0:T(1024)S(1)} %get-tuple-element.9, f32[2048]{0:T(1024)S(1)} %bitcast.53, f32[2048,1792,1,1]{1,0,3,2:T(8,128)} %get-tuple-element.14, f32[]{:T(128)S(6)} %div.46), kind=kLoop, calls=%fused_computation.3 | loop fusion | flops 22020096 | bytes 29375504 | tf_op jit(solution)/shard_map/mul | solution.py:56
  (9 shorter events, 0.0 us)
Async XLA Ops:
  7.2 174.8 %all-gather.5.cloned.1.call-start = ((), (), s32[]{:S(2)}) async-start(), calls=%async_computation.3 | async-start | bytes 5505024 | tf_op jit(solution)/shard_map/all_gather | solution.py:25
  16.3 102.1 %copy-start = (bf16[1,128,4096]{2,1,0:T(8,128)(2,1)S(1)}, bf16[1,128,4096]{2,1,0:T(8,128)(2,1)}, u32[]{:S(2)}) copy-start(bf16[1,128,4096]{2,1,0:T(8,128)(2,1)} %param.6) | copy-start | bytes 3145732
  118.1 143.7 %all-gather.3.cloned.1.call-start = ((), (), s32[]{:S(2)}) async-start(), calls=%async_computation.2 | async-start | bytes 5242880 | tf_op jit(solution)/shard_map/all_gather | solution.py:27
  277.1 58.5 %copy-start.2 = (f32[1,2048]{1,0:T(1,128)S(1)}, f32[1,2048]{1,0:T(1,128)}, u32[]{:S(2)}) copy-start(f32[1,2048]{1,0:T(1,128)} %param.8) | copy-start | bytes 24580
  277.1 65.8 %copy-start.3 = (f32[1,1792]{1,0:T(1,128)S(1)}, f32[1,1792]{1,0:T(1,128)}, u32[]{:S(2)}) copy-start(f32[1,1792]{1,0:T(1,128)} %param.9) | copy-start | bytes 21508
  336.2 48.4 %copy-start.1 = (f32[1,2048]{1,0:T(1,128)}, f32[1,2048]{1,0:T(1,128)S(1)}, u32[]{:S(2)}) copy-start(f32[1,2048]{1,0:T(1,128)S(1)} %get-tuple-element.12) | copy-start | bytes 24580
Sparse Core Ops, SparseCore 0:
  118.3 61.2 all-gather.4
  181.1 80.7 all-gather.2
where the time goes:
time: 392 us; the launch traced here: 391 us
  blocking collectives  152 us (39%)
  other arithmetic  101 us (26%)
  waiting for transfers between devices  79.9 us (20%)
  local copies, waits for them, and re-layouts  26.6 us (7%)
  between operations  16.8 us (4%)
  matrix products  15.2 us (4%)
    all_gather x1, waiting for transfers between devices, body(): shard_rows = lax.all_gather(inputs_split, 'col', axis=1, tiled=True)  79.9 us
    unnamed x2, other arithmetic  63.5 us
    all_to_all x1, blocking collectives, body(): lax.all_to_all(cotangents, 'col', split_axis=2, concat_axis=1, tiled=True)  48.8 us
    psum x1, blocking collectives, body(): squared_total = lax.psum(jnp.sum(squares), ('expert', 'row', 'col'))  38.9 us
    all_to_all x1, blocking collectives, body(): lax.all_to_all(inputs, 'row', split_axis=2, concat_axis=1, tiled=True)  28.1 us
    unnamed x17, local copies, waits for them, and re-layouts  22.7 us
    psum x1, blocking collectives, body(): lax.psum((update_squares, weight_squares), ('row', 'col'))  19.1 us
    dot_general x1, matrix products, body(): jnp.einsum('mkrti,mrktj->mij', input_blocks, hidden_blocks, preferred_ele...  15.2 us
  transfers between devices with their start and end apart: 2, of which 1 were waited for; matrix products, arithmetic and copies ran while one was open for 9% of the time, Pallas kernels for 0%

commit v1 on v0

--- a/solution.py
+++ b/solution.py
@@ -24,7 +24,12 @@
     hidden_split = lax.all_to_all(cotangents, "col", split_axis=2, concat_axis=1, tiled=True)
     hidden_all = lax.all_gather(hidden_split, "row", axis=1, tiled=True)
     hidden_blocks = hidden_all.reshape(matrices, row_count, col_count, block_rows, cols_here)
-    shard_rows = lax.all_gather(inputs_split, "col", axis=1, tiled=True)
+    ring = [inputs_split]
+    for hop in range(3):
+        ring.append(lax.ppermute(ring[-1], "col", [(dev, (dev + 1) % 4) for dev in range(4)]))
+    shard_rows = jnp.roll(
+        jnp.concatenate(ring[::-1], axis=1), (lax.axis_index("col") + 1) * ring[0].shape[1], axis=1
+    )
     block_count = shard_rows.shape[1] // (row_count * block_rows)
     input_blocks = shard_rows.reshape(matrices, block_count, row_count, block_rows, rows_here)
     gradient = jnp.einsum(

time: 392 us -> 375 us (0.957)
  blocking collectives: 152 us -> 75.6 us
  waiting for transfers between devices: 79.9 us -> 111 us
  starting transfers between devices: 0.26 us -> 19.5 us
  local copies, waits for them, and re-layouts: 26.6 us -> 35.9 us
    all_gather x1 -> x0, waiting for transfers between devices: 79.9 us -> none  [body(): shard_rows = lax.all_gather(inputs_split, 'col', axis=1, tiled=True)]
    all_to_all x2 -> x0, blocking collectives: 76.9 us -> none  [the longest x1 48.8 us: body(): lax.all_to_all(cotangents, 'col', split_axis=2, concat_axis=1, tiled=True)]
    ppermute x0 -> x3, waiting for transfers between devices: none -> 71.3 us  [body(): lax.ppermute(ring[-1], 'col', [(dev, (dev + 1) % 4) for dev in range(4)])]
    all_to_all x0 -> x2, waiting for transfers between devices: none -> 23.9 us  [the longest x1 23.9 us: body(): lax.all_to_all(cotangents, 'col', split_axis=2, concat_axis=1, tiled=True)]
    all_gather x1, waiting for transfers between devices: 0.01 us -> 15.4 us  [body(): hidden_all = lax.all_gather(hidden_split, 'row', axis=1, tiled=True)]
    all_to_all x0 -> x2, starting transfers between devices: none -> 9.94 us  [the longest x1 5.68 us: body(): lax.all_to_all(cotangents, 'col', split_axis=2, concat_axis=1, tiled=True)]
    ppermute x0 -> x3, starting transfers between devices: none -> 9.51 us  [body(): lax.ppermute(ring[-1], 'col', [(dev, (dev + 1) % 4) for dev in range(4)])]
    unnamed x17 -> x22, local copies, waits for them, and re-layouts: 22.7 us -> 30.6 us
  transfers between devices with their start and end apart: 2 -> 6, of which waited for: 1 -> 4; matrix products, arithmetic and copies ran while one was open for 9% -> 20% of each run, Pallas kernels for 0% -> 0%
where the time goes in v1:
time: 375 us; the launch traced here: 373 us
  waiting for transfers between devices  111 us (30%)
  other arithmetic  99.6 us (27%)
  blocking collectives  75.6 us (20%)
  local copies, waits for them, and re-layouts  35.9 us (10%)
  starting transfers between devices  19.5 us (5%)
  between operations  16.8 us (4%)
  matrix products  15.2 us (4%)
    ppermute x3, waiting for transfers between devices, body(): lax.ppermute(ring[-1], 'col', [(dev, (dev + 1) % 4) for dev in range(4)])  71.3 us
    unnamed x2, other arithmetic  62.1 us
    psum x1, blocking collectives, body(): squared_total = lax.psum(jnp.sum(squares), ('expert', 'row', 'col'))  39.7 us
    unnamed x22, local copies, waits for them, and re-layouts  30.6 us
    all_to_all x1, waiting for transfers between devices, body(): lax.all_to_all(cotangents, 'col', split_axis=2, concat_axis=1, tiled=True)  23.9 us
    psum x1, blocking collectives, body(): lax.psum((update_squares, weight_squares), ('row', 'col'))  19.1 us
    all_gather x1, waiting for transfers between devices, body(): hidden_all = lax.all_gather(hidden_split, 'row', axis=1, tiled=True)  15.4 us
    dot_general x1, matrix products, body(): jnp.einsum('mkrti,mrktj->mij', input_blocks, hidden_blocks, preferred_ele...  15.2 us
  transfers between devices with their start and end apart: 6, of which 4 were waited for; matrix products, arithmetic and copies ran while one was open for 20% of the time, Pallas kernels for 0%

profile of v1, /device:TPU:0, one launch (start us, length us, event | category | flops | bytes accessed | tf_op | source)
XLA Modules:
  0.0 373.3 jit_solution(15610201608402253185)
XLA Ops:
  7.2 5.0 %copy.16 = bf16[1,128,4096]{1,0,2:T(2,128)(2,1)S(1)} copy(bf16[1,128,4096]{2,1,0:T(8,128)(2,1)} %param.6) | data formatting | bytes 2097152 | tf_op args[1]
  12.7 22.4 %reduce.12 = bf16[4096,128]{1,0:T(8,128)(2,1)S(1)} reduce(bf16[4096,1,128]{2,1,0:T(2,128)(2,1)S(1)} %bitcast.50, bf16[]{:T(256)} %broadcast.18), dimensions={1}, to_apply=%bitcast.39.reduce_sub_computation | reduce | bytes 2097154
  35.1 1.1 reshape.53
  36.3 4.3 %all-to-all-start = ((bf16[2,2,131072]{2,1,0:T(2,128)(2,1)}), bf16[2,2,131072]{2,1,0:T(2,128)(2,1)S(1)}, u32[]{:S(2)}, u32[]{:S(2)}) async-start(bf16[2,2,131072]{2,1,0:T(2,128)(2,1)} %reshape.53), calls=%async_computation | async-start | bytes 2097152 | tf_op jit(solution)/shard_map/all_to_all | solution.py:23
  40.5 8.6 %copy.18 = bf16[1,128,7168]{1,0,2:T(2,128)(2,1)} copy(bf16[1,128,7168]{2,1,0:T(8,128)(2,1)} %param.7) | data formatting | bytes 3670016 | tf_op args[2]
  49.1 39.7 %reduce.13 = bf16[7168,128]{1,0:T(8,128)(2,1)S(1)} reduce(bf16[7168,1,128]{2,1,0:T(2,128)(2,1)} %bitcast.44, bf16[]{:T(256)} %broadcast.18), dimensions={1}, to_apply=%bitcast.41.reduce_sub_computation | reduce | bytes 3670018
  88.9 1.9 reshape.55
  90.8 5.7 %all-to-all-start.1 = ((bf16[4,2,114688]{2,1,0:T(2,128)(2,1)}), bf16[4,2,114688]{2,1,0:T(2,128)(2,1)}, u32[]{:S(2)}, u32[]{:S(2)}) async-start(bf16[4,2,114688]{2,1,0:T(2,128)(2,1)} %reshape.55), calls=%async_computation.1 | async-start | bytes 3670016 | tf_op jit(solution)/shard_map/all_to_all | solution.py:24
  96.5 0.9 reshape.54
  98.1 2.1 collective-permute-start
  100.2 52.7 %collective-permute-done = bf16[1,256,2048]{2,1,0:T(8,128)(2,1)} collective-permute-done((bf16[1,256,2048]{2,1,0:T(8,128)(2,1)S(1)}, bf16[1,256,2048]{2,1,0:T(8,128)(2,1)}, u32[]{:S(2)}, u32[]{:S(2)}) %collective-permute-start) | collective-permute-done | bytes 1048608 | tf_op jit(solution)/shard_map/ppermute | solution.py:29
  152.9 7.4 %collective-permute-start.1 = (bf16[1,256,2048]{2,1,0:T(8,128)(2,1)}, bf16[1,256,2048]{2,1,0:T(8,128)(2,1)}, u32[]{:S(2)}, u32[]{:S(2)}) collective-permute-start(bf16[1,256,2048]{2,1,0:T(8,128)(2,1)} %collective-permute-done), channel_id=1, source_target_pairs={{0,1},{1,2},{2,3},{3,0},{4,5},{5,6},{6,7},{7,4},{8,9},{9,10},{10,1... | collective-permute-start | bytes 3145736 | tf_op jit(solution)/shard_map/ppermute | solution.py:29
  160.2 23.9 %all-to-all-done.1 = bf16[4,2,114688]{2,1,0:T(2,128)(2,1)} async-done(((bf16[4,2,114688]{2,1,0:T(2,128)(2,1)}), bf16[4,2,114688]{2,1,0:T(2,128)(2,1)}, u32[]{:S(2)}, u32[]{:S(2)}) %all-to-all-start.1) | async-done | bytes 1835040 | tf_op jit(solution)/shard_map/all_to_all | solution.py:24
  184.1 4.7 %reshape.56 = bf16[7168,1,128]{2,1,0:T(2,128)(2,1)} reshape(bf16[4,2,114688]{2,1,0:T(2,128)(2,1)} %all-to-all-done.1) | data formatting | bytes 3670016
  188.8 2.3 copy.25
  191.1 2.4 copy.19
  193.6 7.5 %multiply_reduce_fusion.1 = f32[]{:T(128)} fusion(bf16[1,2048,1792]{2,1,0:T(8,128)(2,1)} %param.5), kind=kLoop, calls=%fused_computation.7 | loop fusion | flops 11010047 | bytes 7340036 | tf_op jit(solution)/shard_map/reduce_sum | solution.py:42
  201.2 18.6 %collective-permute-done.2 = bf16[1,256,2048]{2,1,0:T(8,128)(2,1)S(1)} collective-permute-done((bf16[1,256,2048]{2,1,0:T(8,128)(2,1)}, bf16[1,256,2048]{2,1,0:T(8,128)(2,1)S(1)}, u32[]{:S(2)}, u32[]{:S(2)}) %collective-permute-start.2) | collective-permute-done | bytes 1048608 | tf_op jit(solution)/shard_map/ppermute | solution.py:29
  219.9 1.3 constant_dynamic-update-slice_fusion.6
  221.2 1.3 constant_dynamic-update-slice_fusion.5
  222.6 1.3 constant_dynamic-update-slice_fusion.2
  223.9 1.3 constant_dynamic-update-slice_fusion.1
  225.3 2.2 constant_dynamic-slice_fusion
  227.5 15.4 %all-gather.2.cloned.1.call-done = bf16[1,1024,1792]{2,1,0:T(8,128)(2,1)} async-done(((bf16[1,512,1792]{2,1,0:T(8,128)(2,1)}), bf16[1,1024,1792]{2,1,0:T(8,128)(2,1)}) %all-gather.2.cloned.1.call-update) | async-done | bytes 3670032 | tf_op jit(solution)/shard_map/all_gather | solution.py:25
  242.9 15.2 %fusion = (f32[]{:T(128)}, f32[2048,1792,1,1]{1,0,3,2:T(8,128)}) fusion(bf16[4,2,128,2048]{3,2,1,0:T(8,128)(2,1)} %bitcast.54, bf16[2,4,128,1792]{3,2,1,0:T(8,128)(2,1)} %bitcast.58), kind=kOutput, calls=%fused_computation.2 | convolution fusion | flops 7523532800 | bytes 22544388 | tf_op jit(solution)/shard_map/mkrti,mrktj->mij/dot_general | solution.py:35
  258.1 39.7 %psum.43 = f32[]{:T(128)} all-reduce(f32[]{:T(128)} %get-tuple-element.13), channel_id=1, replica_groups=mesh['expert'=4,'row'=2,'col'=4] {'expert','row','col'}, use_global_device_ids=true, to_apply=%region_3.4 | all-reduce | flops 1 | bytes 8 | tf_op jit(solution)/shard_map/psum | solution.py:43
  298.6 8.1 %fusion.1 = (f32[1792]{0:T(1024)S(1)}, f32[2048]{0:T(1024)S(1)}) fusion(f32[2048,1792,1,1]{1,0,3,2:T(8,128)} %get-tuple-element.14, f32[]{:T(128)S(6)} %div.46), kind=kLoop, calls=%fused_computation.8 | loop fusion | flops 18346240 | bytes 14695428 | tf_op jit(solution)/shard_map/reduce_sum | solution.py:50
  306.7 10.8 %psum.44 = f32[1,2048]{1,0:T(1,128)S(1)} all-reduce(f32[1,2048]{1,0:T(1,128)S(1)} %bitcast.57), channel_id=1, replica_groups=mesh['expert'=4,'row'=2,'col'=4] {'col'}, use_global_device_ids=true, to_apply=%region_5.6 | all-reduce | flops 2048 | bytes 16384 | tf_op jit(solution)/shard_map/psum | solution.py:11
  318.1 6.0 %all-reduce.1 = (f32[1]{0:T(128)}, f32[1,1792]{1,0:T(1,128)S(1)}) all-reduce(f32[1]{0:T(128)} %bitcast.12, f32[1,1792]{1,0:T(1,128)S(1)} %reduce_sum.70), channel_id=1, replica_groups=mesh['expert'=4,'row'=2,'col'=4] {'row'}, use_global_device_ids=true, to_apply=%region_9.10 | all-reduce | flops 1793 | bytes 14344 | tf_op jit(solution)/shard_map/psum | solution.py:54
  325.4 8.9 %multiply_reduce_fusion = f32[]{:T(128)} fusion(f32[]{:T(128)} %bitcast.13, f32[1792]{0:T(1024)S(1)} %get-tuple-element.9, f32[2048]{0:T(1024)S(1)} %bitcast.55, f32[2048,1792,1,1]{1,0,3,2:T(8,128)} %get-tuple-element.14, f32[]{:T(128)S(6)} %div.46), kind=kLoop, calls=%fused_computation.4 | loop fusion | flops 22020096 | bytes 14695436 | tf_op jit(solution)/shard_map/reduce_sum | solution.py:57
  334.3 19.1 %all-reduce = (f32[1]{0:T(128)}, f32[1]{0:T(128)}) all-reduce(f32[1]{0:T(128)} %bitcast.14, f32[1]{0:T(128)} %bitcast), channel_id=1, replica_groups=mesh['expert'=4,'row'=2,'col'=4] {'row','col'}, use_global_device_ids=true, to_apply=%region_11.12 | all-reduce | flops 2 | bytes 16 | tf_op jit(solution)/shard_map/psum | solution.py:58
  354.7 11.8 %multiply_bitcast_fusion = f32[1,2048,1792]{2,1,0:T(8,128)} fusion(f32[]{:T(128)} %bitcast.15, f32[]{:T(128)} %bitcast.1, f32[]{:T(128)} %bitcast.13, f32[1792]{0:T(1024)S(1)} %get-tuple-element.9, f32[2048]{0:T(1024)S(1)} %bitcast.56, f32[2048,1792,1,1]{1,0,3,2:T(8,128)} %get-tuple-element.14, f32[]{:T(128)S(6)} %div.46), kind=kLoop, calls=%fused_computation.3 | loop fusion | flops 22020096 | bytes 29375504 | tf_op jit(solution)/shard_map/mul | solution.py:61
  (21 shorter events, 2.8 us)
Async XLA Ops:
  36.3 54.5 %all-to-all-start = ((bf16[2,2,131072]{2,1,0:T(2,128)(2,1)}), bf16[2,2,131072]{2,1,0:T(2,128)(2,1)S(1)}, u32[]{:S(2)}, u32[]{:S(2)}) async-start(bf16[2,2,131072]{2,1,0:T(2,128)(2,1)} %reshape.53), calls=%async_computation | async-start | bytes 2097152 | tf_op jit(solution)/shard_map/all_to_all | solution.py:23
  90.8 93.3 %all-to-all-start.1 = ((bf16[4,2,114688]{2,1,0:T(2,128)(2,1)}), bf16[4,2,114688]{2,1,0:T(2,128)(2,1)}, u32[]{:S(2)}, u32[]{:S(2)}) async-start(bf16[4,2,114688]{2,1,0:T(2,128)(2,1)} %reshape.55), calls=%async_computation.1 | async-start | bytes 3670016 | tf_op jit(solution)/shard_map/all_to_all | solution.py:24
  96.5 146.4 %all-gather.2.cloned.1.call-start = ((), (), s32[]{:S(2)}) async-start(), calls=%async_computation.2 | async-start | bytes 5505024 | tf_op jit(solution)/shard_map/all_gather | solution.py:25
  98.1 54.8 %collective-permute-start = (bf16[1,256,2048]{2,1,0:T(8,128)(2,1)S(1)}, bf16[1,256,2048]{2,1,0:T(8,128)(2,1)}, u32[]{:S(2)}, u32[]{:S(2)}) collective-permute-start(bf16[1,256,2048]{2,1,0:T(8,128)(2,1)S(1)} %bitcast.46), channel_id=1, source_target_pairs={{0,1},{1,2},{2,3},{3,0},{4,5},{5,6},{6,7},{7,4},{8,9},{9,10},{10,1... | collective-permute-start | bytes 3145736 | tf_op jit(solution)/shard_map/ppermute | solution.py:29
  152.9 40.7 %collective-permute-start.1 = (bf16[1,256,2048]{2,1,0:T(8,128)(2,1)}, bf16[1,256,2048]{2,1,0:T(8,128)(2,1)}, u32[]{:S(2)}, u32[]{:S(2)}) collective-permute-start(bf16[1,256,2048]{2,1,0:T(8,128)(2,1)} %collective-permute-done), channel_id=1, source_target_pairs={{0,1},{1,2},{2,3},{3,0},{4,5},{5,6},{6,7},{7,4},{8,9},{9,10},{10,1... | collective-permute-start | bytes 3145736 | tf_op jit(solution)/shard_map/ppermute | solution.py:29
  193.6 26.2 %collective-permute-start.2 = (bf16[1,256,2048]{2,1,0:T(8,128)(2,1)}, bf16[1,256,2048]{2,1,0:T(8,128)(2,1)S(1)}, u32[]{:S(2)}, u32[]{:S(2)}) collective-permute-start(bf16[1,256,2048]{2,1,0:T(8,128)(2,1)} %collective-permute-done.1), channel_id=1, source_target_pairs={{0,1},{1,2},{2,3},{3,0},{4,5},{5,6},{6,7},{7,4},{8,9},{9,10},{10,1... | collective-permute-start | bytes 3145736 | tf_op jit(solution)/shard_map/ppermute | solution.py:29
  258.1 59.3 %copy-start.1 = (f32[1,2048]{1,0:T(1,128)S(1)}, f32[1,2048]{1,0:T(1,128)}, u32[]{:S(2)}) copy-start(f32[1,2048]{1,0:T(1,128)} %param.8) | copy-start | bytes 24580
  258.1 66.6 %copy-start.2 = (f32[1,1792]{1,0:T(1,128)S(1)}, f32[1,1792]{1,0:T(1,128)}, u32[]{:S(2)}) copy-start(f32[1,1792]{1,0:T(1,128)} %param.9) | copy-start | bytes 21508
  318.1 48.4 %copy-start = (f32[1,2048]{1,0:T(1,128)}, f32[1,2048]{1,0:T(1,128)S(1)}, u32[]{:S(2)}) copy-start(f32[1,2048]{1,0:T(1,128)S(1)} %get-tuple-element.12) | copy-start | bytes 24580
Sparse Core Ops, SparseCore 0:
  193.7 49.2 all-gather.1
